TPU v7x, 32 devices: a whole 2x2x4 slice. The times are simulated.
32 devices in a mesh: lat: 8 (over y, x, core), lon: 4 (over z).
Axes of the slice: x: 2, y: 2, z: 4, core: 2. Of those that a mesh axis runs over, the one named last changes fastest.
Arguments:
- right_side: float32 [128, 2560], P('lat', 'lon'), may hold values from -34 to 34
- first_guess: float32 [128, 2560], P('lat', 'lon'), may hold values from -3 to 3
- cell_mask: int32 [128, 2560], P('lat', 'lon'), may hold values 0 or 1
- cond_east: float32 [128, 2560], P('lat', 'lon'), may hold values from 0.5 to 2
- cond_north: float32 [128, 2560], P('lat', 'lon'), may hold values from 0.5 to 2
- surface: float32 [128, 2560], P('lat', 'lon'), may hold values from 0.02 to 0.5
- recycled: float32 [16, 128, 2560], P(None, 'lat', 'lon'), may hold values from -0.0031444706 to 0.0031444706
Outputs:
- solution: float32 [128, 2560], P('lat', 'lon')
- residual: float32 [128, 2560], P('lat', 'lon')
All inputs are finite; a program needn't handle non-finite values. No bound on the sum of `cell_mask` on one device may be relied on, other than what follows from the above.
Results may differ from a plain program's by a relative error of at most 0.0003.
Values sent between devices are 32-bit elements; how exact they have to be, the bound alone decides.
A program may use at most 64 MiB of HBM per device.

v0:
```python
import jax
import jax.numpy as jnp
from jax import lax
from jax.sharding import PartitionSpec as P

ITERS = 3


PRECISE = lax.Precision.HIGHEST


def with_halo(block, sides, width):
    for axis, dim in sides:
        count = lax.axis_size(axis)
        forward = [(i, i + 1) for i in range(count - 1)]
        forward.append((count - 1, 0))
        backward = [(target, source) for source, target in forward]
        low = lax.ppermute(
            lax.slice_in_dim(block, block.shape[dim] - width, None, axis=dim), axis, forward
        )
        high = lax.ppermute(lax.slice_in_dim(block, 0, width, axis=dim), axis, backward)
        block = jnp.concatenate([low, block, high], axis=dim)
    return block


def close_poles(padded):
    row_index = lax.axis_index("lat")
    last_row = lax.axis_size("lat") - 1
    keep_south = (row_index > 0).astype(jnp.float32)
    keep_north = (row_index < last_row).astype(jnp.float32)
    return jnp.concatenate(
        [padded[..., :1, :] * keep_south, padded[..., 1:-1, :], padded[..., -1:, :] * keep_north],
        axis=-2,
    )


def faces(side, surface):
    wet_pad = side[0]
    east_pad = side[1]
    north_pad = side[2]
    wet_cells = wet_pad[1:-1, 1:-1]
    k_east = east_pad[1:-1, 1:-1] * wet_pad[1:-1, 2:]
    k_west = east_pad[1:-1, :-2] * wet_cells
    k_north = north_pad[1:-1, 1:-1] * wet_pad[2:, 1:-1]
    k_south = north_pad[:-2, 1:-1] * wet_cells
    centre = surface * wet_cells + k_east + k_west + k_north + k_south + (1.0 - wet_cells)
    return (centre, k_east, k_west, k_north, k_south)


def operate_padded(padded, coeffs):
    centre, k_east, k_west, k_north, k_south = coeffs
    inner = padded[..., 1:-1, 1:-1]
    to_east = padded[..., 1:-1, 2:]
    to_west = padded[..., 1:-1, :-2]
    to_north = padded[..., 2:, 1:-1]
    to_south = padded[..., :-2, 1:-1]
    return centre * inner - (
        k_east * to_east + k_west * to_west + k_north * to_north + k_south * to_south
    )


def residual_image(residual, coeffs):
    padded = with_halo(residual, (("lat", 0), ("lon", 1)), 1)
    return operate_padded(padded, coeffs)


def solve_small(factor, target):
    return jax.scipy.linalg.cho_solve((factor, True), target)


def shards(right_side, first_guess, cell_mask, cond_east, cond_north, surface, recycled):
    wet_cells = cell_mask.astype(jnp.float32)
    local_side = jnp.stack([wet_cells, cond_east * wet_cells, cond_north * wet_cells, first_guess])
    padded_all = with_halo(
        jnp.concatenate([local_side, recycled], axis=0), (("lat", 1), ("lon", 2)), 1
    )
    side_pad = close_poles(padded_all[:3])
    guess_pad = padded_all[3]
    basis_pad = padded_all[4:]
    coeffs = faces(side_pad, surface)
    basis_image = operate_padded(basis_pad, coeffs)
    start_res = right_side - operate_padded(guess_pad, coeffs)
    gram_local = jnp.einsum("kyx,lyx->kl", recycled, basis_image, precision=PRECISE)
    start_local = jnp.einsum("kyx,yx->k", recycled, start_res, precision=PRECISE)
    gram, start = lax.psum((gram_local, start_local), ("lat", "lon"))
    factor = jnp.linalg.cholesky(0.5 * (gram + gram.T))
    coarse = solve_small(factor, start)
    solution = first_guess + jnp.einsum("kyx,k->yx", recycled, coarse, precision=PRECISE)
    residual = start_res - jnp.einsum("kyx,k->yx", basis_image, coarse, precision=PRECISE)
    direction = residual
    dir_image = residual
    curv = jnp.float32(1.0)
    prev_norm = jnp.float32(1.0)
    for turn_index in range(ITERS):
        image_res = residual_image(residual, coeffs)
        defl_local = jnp.einsum("kyx,yx->k", recycled, image_res, precision=PRECISE)
        res_norm, res_image, defl = lax.psum(
            (jnp.sum(residual * residual), jnp.sum(residual * image_res), defl_local),
            ("lat", "lon"),
        )
        coef = solve_small(factor, defl)
        along_basis = jnp.einsum("kyx,k->yx", recycled, coef, precision=PRECISE)
        along_image = jnp.einsum("kyx,k->yx", basis_image, coef, precision=PRECISE)
        if turn_index == 0:
            direction = residual - along_basis
            dir_image = image_res - along_image
            curv = res_image - jnp.sum(coef * defl)
        else:
            ratio = res_norm / prev_norm
            direction = residual - along_basis + ratio * direction
            dir_image = image_res - along_image + ratio * dir_image
            curv = res_image - jnp.sum(coef * defl) - ratio * ratio * curv
        step_len = res_norm / curv
        solution = solution + step_len * direction
        residual = residual - step_len * dir_image
        prev_norm = res_norm
    return (solution, residual)


def solution(mesh):
    return jax.shard_map(
        shards,
        mesh=mesh,
        in_specs=(
            P("lat", "lon"),
            P("lat", "lon"),
            P("lat", "lon"),
            P("lat", "lon"),
            P("lat", "lon"),
            P("lat", "lon"),
            P(None, "lat", "lon"),
        ),
        out_specs=(P("lat", "lon"), P("lat", "lon")),
        check_vma=False,
    )
```

profile of v0, /device:TPU:0, one launch (start us, length us, event | category | flops | bytes accessed | tf_op | source)
XLA Modules:
  0.0 244.8 jit_solution(5248051123626684629)
XLA Ops:
  4.3 3.4 %collective-permute-start.1 = (f32[20,1,640]{2,1,0:T(1,128)S(1)}, f32[20,1,640]{2,1,0:T(1,128)S(1)}, u32[]{:S(2)}, u32[]{:S(2)}) collective-permute-start(f32[20,1,640]{2,1,0:T(1,128)S(1)} %get-tuple-element.36), channel_id=1, source_target_pairs={{4,0},{8,4},{12,8},{16,12},{20,16},{24,20},{28,24},{0,28},{5,1},{9... | collective-permute-start | bytes 153608 | tf_op jit(solution)/shard_map/ppermute | solution.py:21
  7.7 1.8 collective-permute-done.1
  9.5 2.7 %collective-permute-done = f32[20,1,640]{2,1,0:T(1,128)S(1)} collective-permute-done((f32[20,1,640]{2,1,0:T(1,128)S(1)}, f32[20,1,640]{2,1,0:T(1,128)S(1)}, u32[]{:S(2)}, u32[]{:S(2)}) %collective-permute-start) | collective-permute-done | bytes 51232 | tf_op jit(solution)/shard_map/ppermute | solution.py:18
  12.3 3.7 %collective-permute-start.3 = (f32[20,18,1]{2,1,0:T(8,128)S(1)}, f32[20,18,1]{2,1,0:T(8,128)S(1)}, u32[]{:S(2)}, u32[]{:S(2)}) collective-permute-start(f32[20,18,1]{2,1,0:T(8,128)S(1)} %get-tuple-element.34), channel_id=1, source_target_pairs={{1,0},{2,1},{3,2},{0,3},{5,4},{6,5},{7,6},{4,7},{9,8},{10,9},{11,1... | collective-permute-start | bytes 4328 | tf_op jit(solution)/shard_map/ppermute | solution.py:21
  16.0 5.2 %collective-permute-done.3 = f32[20,18,1]{2,1,0:T(8,128)S(1)} collective-permute-done((f32[20,18,1]{2,1,0:T(8,128)S(1)}, f32[20,18,1]{2,1,0:T(8,128)S(1)}, u32[]{:S(2)}, u32[]{:S(2)}) %collective-permute-start.3) | collective-permute-done | bytes 1472 | tf_op jit(solution)/shard_map/ppermute | solution.py:21
  21.1 3.9 %collective-permute-done.2 = f32[20,18,1]{2,1,0:T(8,128)S(1)} collective-permute-done((f32[20,18,1]{2,1,0:T(8,128)S(1)}, f32[20,18,1]{2,1,0:T(8,128)S(1)}, u32[]{:S(2)}, u32[]{:S(2)}) %collective-permute-start.2) | collective-permute-done | bytes 1472 | tf_op jit(solution)/shard_map/ppermute | solution.py:18
  27.3 1.2 convolution_bitcast_fusion
  29.4 40.8 %all-reduce.3 = (f32[16,16]{0,1:T(8,128)S(1)}, f32[16]{0:T(128)S(1)}) all-reduce(f32[16,16]{0,1:T(8,128)S(1)} %convolution_bitcast_fusion, f32[16]{0:T(128)S(1)} %convolution_bitcast_fusion.9), channel_id=1, replica_groups=mesh['lat'=8,'lon'=4] {'lat','lon'}, use_global_device_ids=true, to_apply=%region_0.0 | all-reduce | flops 272 | bytes 2176 | tf_op jit(solution)/shard_map/psum | solution.py:85
  70.4 1.5 cholesky.18
  73.2 1.2 custom-call.11
  75.4 2.6 %collective-permute-start.5 = (f32[1,640]{1,0:T(1,128)S(1)}, f32[1,640]{1,0:T(1,128)S(1)}, u32[]{:S(2)}, u32[]{:S(2)}) collective-permute-start(f32[1,640]{1,0:T(1,128)S(1)} %get-tuple-element.52), channel_id=1, source_target_pairs={{4,0},{8,4},{12,8},{16,12},{20,16},{24,20},{28,24},{0,28},{5,1},{9... | collective-permute-start | bytes 7688 | tf_op jit(solution)/shard_map/ppermute | solution.py:21
  79.9 3.4 %collective-permute-start.6 = (f32[18,1]{1,0:T(8,128)S(1)}, f32[18,1]{1,0:T(8,128)S(1)}, u32[]{:S(2)}, u32[]{:S(2)}) collective-permute-start(f32[18,1]{1,0:T(8,128)S(1)} %get-tuple-element.44), channel_id=1, source_target_pairs={{1,0},{2,1},{3,2},{0,3},{5,4},{6,5},{7,6},{4,7},{9,8},{10,9},{11,1... | collective-permute-start | bytes 224 | tf_op jit(solution)/shard_map/ppermute | solution.py:21
  83.3 1.7 collective-permute-done.7
  86.6 39.8 %all-reduce.2 = (f32[]{:T(128)}, f32[]{:T(128)}, f32[16]{0:T(128)S(1)}) all-reduce(f32[]{:T(128)} %get-tuple-element.8, f32[]{:T(128)} %get-tuple-element.7, f32[16]{0:T(128)S(1)} %convolution_bitcast_fusion.6), channel_id=1, replica_groups=mesh['lat'=8,'lon'=4] {'lat','lon'}, use_global_device_ids=true, to_apply=%region_5.7 | all-reduce | flops 18 | bytes 144 | tf_op jit(solution)/shard_map/psum | solution.py:97
  130.0 2.6 %collective-permute-start.9 = (f32[1,640]{1,0:T(1,128)S(1)}, f32[1,640]{1,0:T(1,128)S(1)}, u32[]{:S(2)}, u32[]{:S(2)}) collective-permute-start(f32[1,640]{1,0:T(1,128)S(1)} %get-tuple-element.50), channel_id=1, source_target_pairs={{4,0},{8,4},{12,8},{16,12},{20,16},{24,20},{28,24},{0,28},{5,1},{9... | collective-permute-start | bytes 7688 | tf_op jit(solution)/shard_map/ppermute | solution.py:21
  134.0 2.1 collective-permute-start.11
  136.1 1.7 collective-permute-start.10
  137.8 1.7 collective-permute-done.11
  141.5 40.9 %all-reduce.1 = (f32[16]{0:T(128)S(1)}, f32[]{:T(128)}, f32[]{:T(128)}) all-reduce(f32[16]{0:T(128)S(1)} %convolution_bitcast_fusion.4, f32[]{:T(128)} %get-tuple-element.6, f32[]{:T(128)} %get-tuple-element.5), channel_id=1, replica_groups=mesh['lat'=8,'lon'=4] {'lat','lon'}, use_global_device_ids=true, to_apply=%region_14.16 | all-reduce | flops 18 | bytes 144 | tf_op jit(solution)/shard_map/psum | solution.py:97
  187.4 2.6 %collective-permute-start.13 = (f32[1,640]{1,0:T(1,128)S(1)}, f32[1,640]{1,0:T(1,128)S(1)}, u32[]{:S(2)}, u32[]{:S(2)}) collective-permute-start(f32[1,640]{1,0:T(1,128)S(1)} %get-tuple-element.48), channel_id=1, source_target_pairs={{4,0},{8,4},{12,8},{16,12},{20,16},{24,20},{28,24},{0,28},{5,1},{9... | collective-permute-start | bytes 7688 | tf_op jit(solution)/shard_map/ppermute | solution.py:21
  191.4 1.9 collective-permute-start.15
  193.3 1.9 collective-permute-start.14
  195.3 1.7 collective-permute-done.15
  198.7 39.9 %all-reduce = (f32[16]{0:T(128)S(1)}, f32[]{:T(128)}, f32[]{:T(128)}) all-reduce(f32[16]{0:T(128)S(1)} %convolution_bitcast_fusion.2, f32[]{:T(128)} %get-tuple-element.4, f32[]{:T(128)} %get-tuple-element.3), channel_id=1, replica_groups=mesh['lat'=8,'lon'=4] {'lat','lon'}, use_global_device_ids=true, to_apply=%region_20.22 | all-reduce | flops 18 | bytes 144 | tf_op jit(solution)/shard_map/psum | solution.py:97
  (81 shorter events, 25.5 us)
Async XLA Ops:
  0.6 0.9 copy-start.1
  0.6 0.9 copy-start.5
  1.5 0.8 copy-start.6
  2.3 0.8 copy-start.2
  4.3 5.2 %collective-permute-start.1 = (f32[20,1,640]{2,1,0:T(1,128)S(1)}, f32[20,1,640]{2,1,0:T(1,128)S(1)}, u32[]{:S(2)}, u32[]{:S(2)}) collective-permute-start(f32[20,1,640]{2,1,0:T(1,128)S(1)} %get-tuple-element.36), channel_id=1, source_target_pairs={{4,0},{8,4},{12,8},{16,12},{20,16},{24,20},{28,24},{0,28},{5,1},{9... | collective-permute-start | bytes 153608 | tf_op jit(solution)/shard_map/ppermute | solution.py:21
  7.7 4.4 %collective-permute-start = (f32[20,1,640]{2,1,0:T(1,128)S(1)}, f32[20,1,640]{2,1,0:T(1,128)S(1)}, u32[]{:S(2)}, u32[]{:S(2)}) collective-permute-start(f32[20,1,640]{2,1,0:T(1,128)S(1)} %get-tuple-element.35), channel_id=1, source_target_pairs={{0,4},{4,8},{8,12},{12,16},{16,20},{20,24},{24,28},{28,0},{1,5},{5... | collective-permute-start | bytes 153608 | tf_op jit(solution)/shard_map/ppermute | solution.py:18
  12.3 8.8 %collective-permute-start.3 = (f32[20,18,1]{2,1,0:T(8,128)S(1)}, f32[20,18,1]{2,1,0:T(8,128)S(1)}, u32[]{:S(2)}, u32[]{:S(2)}) collective-permute-start(f32[20,18,1]{2,1,0:T(8,128)S(1)} %get-tuple-element.34), channel_id=1, source_target_pairs={{1,0},{2,1},{3,2},{0,3},{5,4},{6,5},{7,6},{4,7},{9,8},{10,9},{11,1... | collective-permute-start | bytes 4328 | tf_op jit(solution)/shard_map/ppermute | solution.py:21
  16.0 9.1 %collective-permute-start.2 = (f32[20,18,1]{2,1,0:T(8,128)S(1)}, f32[20,18,1]{2,1,0:T(8,128)S(1)}, u32[]{:S(2)}, u32[]{:S(2)}) collective-permute-start(f32[20,18,1]{2,1,0:T(8,128)S(1)} %get-tuple-element.33), channel_id=1, source_target_pairs={{0,1},{1,2},{2,3},{3,0},{4,5},{5,6},{6,7},{7,4},{8,9},{9,10},{10,1... | collective-permute-start | bytes 4328 | tf_op jit(solution)/shard_map/ppermute | solution.py:18
  25.4 0.8 copy-start.3
  25.4 0.8 copy-start.4
  25.5 1.1 copy-start
  75.4 4.0 %collective-permute-start.4 = (f32[1,640]{1,0:T(1,128)S(1)}, f32[1,640]{1,0:T(1,128)S(1)}, u32[]{:S(2)}, u32[]{:S(2)}) collective-permute-start(f32[1,640]{1,0:T(1,128)S(1)} %get-tuple-element.53), channel_id=1, source_target_pairs={{0,4},{4,8},{8,12},{12,16},{16,20},{20,24},{24,28},{28,0},{1,5},{5... | collective-permute-start | bytes 7688 | tf_op jit(solution)/shard_map/ppermute | solution.py:18
  75.4 3.9 %collective-permute-start.5 = (f32[1,640]{1,0:T(1,128)S(1)}, f32[1,640]{1,0:T(1,128)S(1)}, u32[]{:S(2)}, u32[]{:S(2)}) collective-permute-start(f32[1,640]{1,0:T(1,128)S(1)} %get-tuple-element.52), channel_id=1, source_target_pairs={{4,0},{8,4},{12,8},{16,12},{20,16},{24,20},{28,24},{0,28},{5,1},{9... | collective-permute-start | bytes 7688 | tf_op jit(solution)/shard_map/ppermute | solution.py:21
  79.5 5.5 %collective-permute-start.7 = (f32[18,1]{1,0:T(8,128)S(1)}, f32[18,1]{1,0:T(8,128)S(1)}, u32[]{:S(2)}, u32[]{:S(2)}) collective-permute-start(f32[18,1]{1,0:T(8,128)S(1)} %get-tuple-element.45), channel_id=1, source_target_pairs={{0,1},{1,2},{2,3},{3,0},{4,5},{5,6},{6,7},{7,4},{8,9},{9,10},{10,1... | collective-permute-start | bytes 224 | tf_op jit(solution)/shard_map/ppermute | solution.py:18
  79.9 5.1 %collective-permute-start.6 = (f32[18,1]{1,0:T(8,128)S(1)}, f32[18,1]{1,0:T(8,128)S(1)}, u32[]{:S(2)}, u32[]{:S(2)}) collective-permute-start(f32[18,1]{1,0:T(8,128)S(1)} %get-tuple-element.44), channel_id=1, source_target_pairs={{1,0},{2,1},{3,2},{0,3},{5,4},{6,5},{7,6},{4,7},{9,8},{10,9},{11,1... | collective-permute-start | bytes 224 | tf_op jit(solution)/shard_map/ppermute | solution.py:21
  129.9 4.0 %collective-permute-start.8 = (f32[1,640]{1,0:T(1,128)S(1)}, f32[1,640]{1,0:T(1,128)S(1)}, u32[]{:S(2)}, u32[]{:S(2)}) collective-permute-start(f32[1,640]{1,0:T(1,128)S(1)} %get-tuple-element.51), channel_id=1, source_target_pairs={{0,4},{4,8},{8,12},{12,16},{16,20},{20,24},{24,28},{28,0},{1,5},{5... | collective-permute-start | bytes 7688 | tf_op jit(solution)/shard_map/ppermute | solution.py:18
  130.0 3.9 %collective-permute-start.9 = (f32[1,640]{1,0:T(1,128)S(1)}, f32[1,640]{1,0:T(1,128)S(1)}, u32[]{:S(2)}, u32[]{:S(2)}) collective-permute-start(f32[1,640]{1,0:T(1,128)S(1)} %get-tuple-element.50), channel_id=1, source_target_pairs={{4,0},{8,4},{12,8},{16,12},{20,16},{24,20},{28,24},{0,28},{5,1},{9... | collective-permute-start | bytes 7688 | tf_op jit(solution)/shard_map/ppermute | solution.py:21
  134.0 5.5 %collective-permute-start.11 = (f32[18,1]{1,0:T(8,128)S(1)}, f32[18,1]{1,0:T(8,128)S(1)}, u32[]{:S(2)}, u32[]{:S(2)}) collective-permute-start(f32[18,1]{1,0:T(8,128)S(1)} %get-tuple-element.43), channel_id=1, source_target_pairs={{0,1},{1,2},{2,3},{3,0},{4,5},{5,6},{6,7},{7,4},{8,9},{9,10},{10,1... | collective-permute-start | bytes 224 | tf_op jit(solution)/shard_map/ppermute | solution.py:18
  136.1 3.7 %collective-permute-start.10 = (f32[18,1]{1,0:T(8,128)S(1)}, f32[18,1]{1,0:T(8,128)S(1)}, u32[]{:S(2)}, u32[]{:S(2)}) collective-permute-start(f32[18,1]{1,0:T(8,128)S(1)} %get-tuple-element.42), channel_id=1, source_target_pairs={{1,0},{2,1},{3,2},{0,3},{5,4},{6,5},{7,6},{4,7},{9,8},{10,9},{11,1... | collective-permute-start | bytes 224 | tf_op jit(solution)/shard_map/ppermute | solution.py:21
  187.3 4.0 %collective-permute-start.12 = (f32[1,640]{1,0:T(1,128)S(1)}, f32[1,640]{1,0:T(1,128)S(1)}, u32[]{:S(2)}, u32[]{:S(2)}) collective-permute-start(f32[1,640]{1,0:T(1,128)S(1)} %get-tuple-element.49), channel_id=1, source_target_pairs={{0,4},{4,8},{8,12},{12,16},{16,20},{20,24},{24,28},{28,0},{1,5},{5... | collective-permute-start | bytes 7688 | tf_op jit(solution)/shard_map/ppermute | solution.py:18
  187.4 3.9 %collective-permute-start.13 = (f32[1,640]{1,0:T(1,128)S(1)}, f32[1,640]{1,0:T(1,128)S(1)}, u32[]{:S(2)}, u32[]{:S(2)}) collective-permute-start(f32[1,640]{1,0:T(1,128)S(1)} %get-tuple-element.48), channel_id=1, source_target_pairs={{4,0},{8,4},{12,8},{16,12},{20,16},{24,20},{28,24},{0,28},{5,1},{9... | collective-permute-start | bytes 7688 | tf_op jit(solution)/shard_map/ppermute | solution.py:21
  191.4 5.5 %collective-permute-start.15 = (f32[18,1]{1,0:T(8,128)S(1)}, f32[18,1]{1,0:T(8,128)S(1)}, u32[]{:S(2)}, u32[]{:S(2)}) collective-permute-start(f32[18,1]{1,0:T(8,128)S(1)} %get-tuple-element.41), channel_id=1, source_target_pairs={{0,1},{1,2},{2,3},{3,0},{4,5},{5,6},{6,7},{7,4},{8,9},{9,10},{10,1... | collective-permute-start | bytes 224 | tf_op jit(solution)/shard_map/ppermute | solution.py:18
  193.3 3.7 %collective-permute-start.14 = (f32[18,1]{1,0:T(8,128)S(1)}, f32[18,1]{1,0:T(8,128)S(1)}, u32[]{:S(2)}, u32[]{:S(2)}) collective-permute-start(f32[18,1]{1,0:T(8,128)S(1)} %get-tuple-element.40), channel_id=1, source_target_pairs={{1,0},{2,1},{3,2},{0,3},{5,4},{6,5},{7,6},{4,7},{9,8},{10,9},{11,1... | collective-permute-start | bytes 224 | tf_op jit(solution)/shard_map/ppermute | solution.py:21
where the time goes:
time: 246 us; the launch traced here: 245 us
  blocking collectives  161 us (65%)
  starting transfers between devices  26.6 us (11%)
  waiting for transfers between devices  21.1 us (9%)
  matrix products  13 us (5%)
  other arithmetic  9.43 us (4%)
  between operations  9.36 us (4%)
  local copies, waits for them, and re-layouts  3.82 us (2%)
    psum x3, blocking collectives, shards(): lax.psum((jnp.sum(residual * residual), jnp.sum(residual * image_res), de...  121 us
    psum x1, blocking collectives, shards(): gram, start = lax.psum((gram_local, start_local), ('lat', 'lon'))  40.8 us
    ppermute x8, starting transfers between devices, with_halo(): lax.ppermute(lax.slice_in_dim(block, 0, width, axis=dim), axis, backward)  22 us
    ppermute x8, waiting for transfers between devices, with_halo(): lax.ppermute(lax.slice_in_dim(block, block.shape[dim] - width, None, axis...  13.5 us
    ppermute x8, waiting for transfers between devices, with_halo(): lax.ppermute(lax.slice_in_dim(block, 0, width, axis=dim), axis, backward)  7.51 us
  transfers between devices with their start and end apart: 16, of which 12 were waited for; matrix products, arithmetic and copies ran while one was open for 1% of the time, Pallas kernels for 0%

commit v1 on v0

v1 whole, which is shorter than its diff:
```python
import functools

import jax
import jax.numpy as jnp
from jax import lax
from jax.experimental import pallas as pl
from jax.experimental.pallas import tpu as pltpu
from jax.sharding import PartitionSpec as P

MESH = pl.DeviceIdType.MESH
ITERS = 3
H = 4
F32 = jnp.float32
THETA = 5.5


def kernel(
    n_lat, n_lon, K, R, C,
    b_hbm, x0_hbm, mask_hbm, ce_hbm, cn_hbm, surf_hbm, w_hbm,
    x_out, r_out,
    stage_w, st_b, st_x0, st_mask, st_ce, st_cn, st_surf,
    ext, zbuf, coef, pack, packs_in, part, red1, red2,
    load_sem, send_sem, recv_sem, s1_send, s1_recv, s2_send, s2_recv,
):
    lat = lax.axis_index("lat")
    lon = lax.axis_index("lon")
    RE = R + 2 * H
    CE = C + 128
    S = 24
    NL = H + 1
    Z = NL * K + 16
    has_n = lat < n_lat - 1
    has_s = lat > 0
    east = lax.rem(lon + 1, n_lon)
    west = lax.rem(lon + n_lon - 1, n_lon)

    loads = []
    pairs = tuple(
        (w_hbm.at[:, pl.ds(128 * t, 128)], stage_w.at[t]) for t in range(C // 128)
    ) + (
        (b_hbm, st_b), (x0_hbm, st_x0), (mask_hbm, st_mask),
        (ce_hbm, st_ce), (cn_hbm, st_cn), (surf_hbm, st_surf),
    )
    for i, (src, dst) in enumerate(pairs):
        c = pltpu.make_async_copy(src, dst, load_sem.at[i])
        c.start()
        loads.append(c)

    barrier = pltpu.get_barrier_semaphore()

    def greet_lat(d, _):
        pl.semaphore_signal(barrier, inc=1, device_id=(lax.rem(lat + d, n_lat), lon), device_id_type=MESH)
        return 0

    def greet_lon(d, _):
        pl.semaphore_signal(barrier, inc=1, device_id=(lat, lax.rem(lon + d, n_lon)), device_id_type=MESH)
        return 0

    lax.fori_loop(1, n_lat, greet_lat, 0)
    lax.fori_loop(1, n_lon, greet_lon, 0)

    @pl.when(has_n)
    def _():
        for t in (east, west):
            pl.semaphore_signal(barrier, inc=1, device_id=(lat + 1, t), device_id_type=MESH)

    @pl.when(has_s)
    def _():
        for t in (east, west):
            pl.semaphore_signal(barrier, inc=1, device_id=(lat - 1, t), device_id_type=MESH)

    for c in loads:
        c.wait()

    for t in range(C // 128):
        ln = pl.ds(128 * t, 128)
        for y in range(R):
            v = stage_w[t, pl.ds(y, K, stride=R), :]
            ext[t, pl.ds(S * y, K), :] = v
            zbuf[t, pl.ds(Z * y, K), :] = v
        fields = (
            st_x0[:, ln], st_b[:, ln], st_mask[:, ln].astype(F32), st_ce[:, ln], st_cn[:, ln], st_surf[:, ln],
        )
        for f, v in enumerate(fields):
            ext[t, pl.ds(K + f, R, stride=S), :] = v
        for f in range(K + 6, S):
            ext[t, pl.ds(f, R, stride=S), :] = jnp.zeros((R, 128), F32)

    lane_s = lax.broadcasted_iota(jnp.int32, (S, 128), 1)
    acc = jnp.zeros((S, 128), F32)
    half = 64
    for y in range(R):
        lo = ext[0, pl.ds(S * y, S), :]
        hi = ext[C // 128 - 1, pl.ds(S * y, S), :]
        a0 = H * y
        if a0:
            lo = pltpu.roll(lo, a0, 1)
        hi = pltpu.roll(hi, (half + a0 + H - 128) % 128, 1)
        acc = jnp.where((lane_s >= a0) & (lane_s < a0 + H), lo, acc)
        acc = jnp.where((lane_s >= half + a0) & (lane_s < half + a0 + H), hi, acc)
    pack[...] = acc

    side = has_n.astype(jnp.int32) + has_s.astype(jnp.int32)
    pl.semaphore_wait(barrier, (n_lat - 1) + (n_lon - 1) + 2 * side)

    own = pl.ds(0, C // 128)

    def copy(src, dst, i, dev):
        return pltpu.make_async_remote_copy(
            src_ref=src, dst_ref=dst, send_sem=send_sem.at[i], recv_sem=recv_sem.at[i],
            device_id=dev, device_id_type=MESH,
        )

    to_n = (
        copy(ext.at[own, pl.ds(S * (R - H), S * H)], ext.at[own, pl.ds(S * (R + H), S * H)], 0, (lat + 1, lon)),
        copy(pack, packs_in.at[2], 4, (lat + 1, east)),
        copy(pack, packs_in.at[3], 5, (lat + 1, west)),
    )
    to_s = (
        copy(ext.at[own, pl.ds(0, S * H)], ext.at[own, pl.ds(S * R, S * H)], 1, (lat - 1, lon)),
        copy(pack, packs_in.at[4], 6, (lat - 1, east)),
        copy(pack, packs_in.at[5], 7, (lat - 1, west)),
    )
    to_e = copy(pack, packs_in.at[0], 2, (lat, east))
    to_w = copy(pack, packs_in.at[1], 3, (lat, west))

    to_e.start()
    to_w.start()

    @pl.when(has_n)
    def _():
        for c in to_n:
            c.start()

    @pl.when(has_s)
    def _():
        for c in to_s:
            c.start()

    to_e.wait()
    to_w.wait()

    @pl.when(has_n)
    def _():
        for c in to_n:
            c.wait_send()
        for c in to_s:
            c.wait_recv()

    @pl.when(has_s)
    def _():
        for c in to_s:
            c.wait_send()
        for c in to_n:
            c.wait_recv()

    @pl.when(jnp.logical_not(has_n))
    def _():
        ext[:, pl.ds(S * R, S * H), :] = jnp.zeros((CE // 128, S * H, 128), F32)

    @pl.when(jnp.logical_not(has_s))
    def _():
        ext[:, pl.ds(S * (R + H), S * H), :] = jnp.zeros((CE // 128, S * H, 128), F32)

    def unpack(y_ext, y_src, west_slot, east_slot, keep):
        from_e = packs_in[east_slot]
        from_w = packs_in[west_slot]
        e = pltpu.roll(from_e, (128 - H * y_src) % 128, 1) if y_src else from_e
        w = pltpu.roll(from_w, (128 - H - half - H * y_src) % 128, 1)
        v = jnp.where(lane_s < H, e, jnp.where(lane_s >= 128 - H, w, 0.0))
        if keep is not None:
            v = jnp.where(keep, v, 0.0)
        ext[C // 128, pl.ds(S * y_ext, S), :] = v

    for y in range(R):
        unpack(y, y, 0, 1, None)
    for y in range(H):
        unpack(R + y, y, 4, 5, has_n)
        unpack(R + H + y, R - H + y, 2, 3, has_s)

    def field(f):
        return jnp.concatenate(
            [ext[t, pl.ds(K + f, RE, stride=S), :] for t in range(CE // 128)], axis=1
        )

    def e_of(v):
        return pltpu.roll(v, CE - 1, 1)

    def w_of(v):
        return pltpu.roll(v, 1, 1)

    def n_of(v):
        return pltpu.roll(v, RE - 1, 0)

    def s_of(v):
        return pltpu.roll(v, 1, 0)

    x0 = field(0)
    rhs = field(1)
    wet = field(2)
    cew = field(3) * wet
    cnw = field(4) * wet
    k_e = cew * e_of(wet)
    k_w = w_of(cew) * wet
    k_n = cnw * n_of(wet)
    k_s = s_of(cnw) * wet
    centre = field(5) * wet + k_e + k_w + k_n + k_s + (1.0 - wet)
    for i, v in enumerate((centre, k_e, k_w, k_n, k_s)):
        coef[i] = v

    def operate(v):
        return centre * v - (k_e * e_of(v) + k_w * w_of(v) + k_n * n_of(v) + k_s * s_of(v))

    s_fam = [rhs - operate(x0)]
    for _ in range(ITERS):
        s_fam.append(operate(s_fam[-1]) - THETA * s_fam[-1])
    for t in range(C // 128):
        ln = pl.ds(128 * t, 128)
        for i, v in enumerate(s_fam):
            p = v[:R, 128 * t:128 * t + 128]
            p_hi = p.astype(jnp.bfloat16).astype(F32)
            zbuf[t, pl.ds(NL * K + i, R, stride=Z), :] = p_hi
            zbuf[t, pl.ds(NL * K + 4 + i, R, stride=Z), :] = p - p_hi
        for i in range(8, 16):
            zbuf[t, pl.ds(NL * K + i, R, stride=Z), :] = jnp.zeros((R, 128), F32)

    def rows(ref, level, y):
        start = S * y if level == 0 else Z * y + level * K
        at = pl.ds(pl.multiple_of(start, 8), K)
        return jnp.concatenate([ref[t, at, :] for t in range(CE // 128)], axis=1)

    for level in range(1, NL):
        h = NL - 1 - level
        src = ext if level == 1 else zbuf

        def body(t, _, level=level, h=h, src=src):
            y = lax.rem(t + (RE - h), RE)
            yn = lax.rem(y + 1, RE)
            ys = lax.rem(y + RE - 1, RE)
            v = rows(src, level - 1, y)
            vn = rows(src, level - 1, yn)
            vs = rows(src, level - 1, ys)

            def kk(i):
                return coef[i, pl.ds(y, 1), :]

            diag = kk(0) if level == 1 else kk(0) - THETA
            out = diag * v - (kk(1) * e_of(v) + kk(2) * w_of(v) + kk(3) * vn + kk(4) * vs)
            at = pl.ds(pl.multiple_of(Z * y + level * K, 8), K)
            for u in range(CE // 128):
                zbuf[u, at, :] = out[:, 128 * u:128 * u + 128]
            return 0

        lax.fori_loop(0, R + 2 * h, body, 0)

    def gram_step(t, total):
        z = jnp.concatenate(
            [
                zbuf[q, pl.ds(pl.multiple_of(Z * (2 * t + u), 8), Z), :]
                for u in range(2) for q in range(C // 128)
            ],
            axis=1,
        )
        hi = z.astype(jnp.bfloat16)
        lo = (z - hi.astype(F32)).astype(jnp.bfloat16)
        both = jnp.concatenate([hi, lo[:NL * K]], axis=0)
        return total + lax.dot_general(
            both, both, (((1,), (1,)), ((), ())), preferred_element_type=F32
        )

    G = lax.fori_loop(0, R // 2, gram_step, jnp.zeros((Z + NL * K, Z + NL * K), F32))
    zl = jnp.zeros((Z + NL * K, 256 - Z - NL * K), F32)
    G = jnp.concatenate([G, zl], axis=1)
    GL = pltpu.roll(G, 256 - Z, 1)[:, :128]
    G = G[:, :128]

    lane = lax.broadcasted_iota(jnp.int32, (K, 128), 1)
    sub = lax.broadcasted_iota(jnp.int32, (K, 128), 0)

    def moved(v, src, dst):
        s = (dst - src) % 128
        return pltpu.roll(v, s, 1) if s else v

    SB = NL * K
    NM = 2 * ITERS + 1
    AB = NM * K
    P_ = jnp.zeros((K, 128), F32)
    for m in range(1, NM + 1):
        i = m // 2
        j = m - i
        hh = G[i * K:(i + 1) * K] + G[Z + i * K:Z + (i + 1) * K]
        hl = GL[i * K:(i + 1) * K] + GL[Z + i * K:Z + (i + 1) * K]
        dst = (m - 1) * K
        v = moved(hh + hl, j * K, dst)
        P_ = jnp.where((lane >= dst) & (lane < dst + K), v, P_)
    for m in range(NM):
        j = m // 2
        i = m - j
        hh = G[i * K:(i + 1) * K] + G[Z + i * K:Z + (i + 1) * K]
        v = moved(hh, SB + j, AB + m) + moved(hh, SB + 4 + j, AB + m)
        P_ = jnp.where(lane == AB + m, v, P_)
    SL = AB + NM
    for m in range(2 * ITERS):
        i = m // 2
        j = m - i
        g = G[SB:SB + 8]
        v = moved(g, SB + j, SL) + moved(g, SB + 4 + j, SL)
        P_ = jnp.where((lane == SL) & (sub == m), v[i:i + 1] + v[4 + i:5 + i], P_)
    part[...] = P_

    def exchange(src, slots, send, recv, n, me, dev):
        def desc(d):
            return pltpu.make_async_remote_copy(
                src_ref=src, dst_ref=slots.at[me], send_sem=send.at[d], recv_sem=recv.at[me],
                device_id=dev(lax.rem(me + d, n)), device_id_type=MESH,
            )

        def from_slot(d):
            slot = lax.rem(me + d, n)
            return pltpu.make_async_remote_copy(
                src_ref=src, dst_ref=slots.at[slot], send_sem=send.at[d], recv_sem=recv.at[slot],
                device_id=dev(slot), device_id_type=MESH,
            )

        def start(d, _):
            desc(d).start()
            return 0

        def finish(d, _):
            desc(d).wait_send()
            from_slot(d).wait_recv()
            return 0

        lax.fori_loop(1, n, start, 0)
        slots[me] = src[...]
        lax.fori_loop(1, n, finish, 0)
        return lax.fori_loop(0, n, lambda d, t: t + slots[d], jnp.zeros((K, 128), F32))

    part[...] = exchange(part, red1, s1_send, s1_recv, n_lat, lat, lambda o: (o, lon))
    M = exchange(part, red2, s2_send, s2_recv, n_lon, lon, lambda o: (lat, o))

    MT = M.T
    sym = M
    for m in range(NM):
        t = MT[m * K:(m + 1) * K]
        t = jnp.concatenate([t, jnp.zeros((K, 128 - K), F32)], axis=1)
        t = moved(t, 0, m * K)
        sym = jnp.where((lane >= m * K) & (lane < (m + 1) * K), 0.5 * (M + t), sym)

    Q = sym
    for k in range(K):
        column = jnp.broadcast_to(Q[:, k:k + 1], (K, 128))
        pivot = column[k:k + 1]
        unit = (sub == k).astype(F32)
        Q = jnp.where(lane == k, unit, Q)
        Q = Q - (column - unit) * (Q[k:k + 1] / pivot)

    def col(v, m):
        return jnp.sum(jnp.where(lane == (m - 1) * K + sub, v, 0.0), axis=1, keepdims=True)

    def row_of(v):
        return jnp.sum(Q * v, axis=0, keepdims=True)

    def tiled(v):
        return jnp.sum(jnp.where(lax.rem(lane, K) == sub, v, 0.0), axis=0, keepdims=True)

    lane8 = lax.broadcasted_iota(jnp.int32, (8, 128), 1)
    sub8 = lax.broadcasted_iota(jnp.int32, (8, 128), 0)
    seg_mask = lane8 // K == sub8

    def seg_dots(t, v):
        d = jnp.sum(jnp.where(seg_mask, t * v, 0.0), axis=1, keepdims=True)
        return lambda m: d[m - 1:m]

    a = [sym[:, AB + m:AB + m + 1] for m in range(NM)]
    sigma = [M[m:m + 1, SL:SL + 1] for m in range(2 * ITERS)]

    U = row_of(a[0])
    c = col(U, 1)
    cu = seg_dots(tiled(c), U)
    b = [None] + [a[m] - col(U, m + 1) for m in range(1, 4)]
    sg = [sigma[m] - 2.0 * U[:, AB + m + 1:AB + m + 2] + cu(m + 2) for m in range(2 * ITERS)]

    def products(v):
        r = row_of(v)
        q = col(r, 1)
        qt = tiled(q)
        qu = seg_dots(qt, U)
        qb = lambda m: r[:, AB + m:AB + m + 1] - qu(m + 1)
        return r, q, qt, qb

    zero = jnp.zeros((1, 1), F32)

    def norm2(f, gx, gy, gz, e):
        t = gx * gx * q0v(2 + e)
        for i in range(len(f)):
            for k in range(len(f)):
                t = t + f[i] * f[k] * sg[i + k + e]
            t = t + 2.0 * f[i] * gx * q0b(i + 1 + e)
            if gz is not None:
                t = t + 2.0 * f[i] * (gy * q1b(i + 1 + e) + gz * q0b(i + 2 + e))
        if gz is not None:
            t = t + 2.0 * gx * gy * q1v(2 + e) + gy * gy * q1w(2 + e)
            t = t + 2.0 * gz * (gx * q0v(3 + e) + gy * q1v(3 + e)) + gz * gz * q0v(4 + e)
        return t

    V, q0, q0t, q0b = products(b[1])
    q0v = seg_dots(q0t, V)
    v2, v3 = col(V, 2), col(V, 3)
    rn0 = sg[0]
    rz0 = sg[1] + THETA * rn0
    curv0 = rz0 - q0b(1)
    al0 = rn0 / curv0
    f = [1.0 - al0 * THETA, -al0]
    d1 = f[0] * b[1] + f[1] * b[2] + al0 * v2
    Wr, q1, q1t, q1b = products(d1)
    q1v = seg_dots(q1t, V)
    q1w = seg_dots(q1t, Wr)
    w2 = col(Wr, 2)
    rn1 = norm2(f, al0, None, None, 0)
    rz1 = norm2(f, al0, None, None, 1) + THETA * rn1
    be1 = rn1 / rn0
    curv1 = rz1 - jnp.sum(q1 * d1, axis=0, keepdims=True) - be1 * be1 * curv0
    al1 = rn1 / curv1
    gx = al0 - al1 * (THETA * al0 - be1)
    gy = al1
    gz = -al1 * al0
    f = [
        f[0] - al1 * THETA * (f[0] + be1),
        f[1] - al1 * (f[0] + THETA * f[1] + be1),
        -al1 * f[1],
    ]
    d2 = f[0] * b[1] + f[1] * b[2] + f[2] * b[3] + gx * v2 + gy * w2 + gz * v3
    rn2 = norm2(f, gx, gy, gz, 0)
    rz2 = norm2(f, gx, gy, gz, 1) + THETA * rn2
    be2 = rn2 / rn1
    q2 = col(row_of(d2), 1)
    curv2 = rz2 - jnp.sum(q2 * d2, axis=0, keepdims=True) - be2 * be2 * curv1
    al2 = rn2 / curv2

    zc = jnp.zeros((K, 1), F32)

    def combine(x, scale, y):
        n = max(len(x[0]), len(y[0]))
        pad = lambda l, z0, k: list(l) + [z0] * (k - len(l))
        fx, fy = pad(x[0], zero, n), pad(y[0], zero, n)
        m = max(len(x[1]), len(y[1]))
        gx_, gy_ = pad(x[1], zc, m), pad(y[1], zc, m)
        return [p + scale * q for p, q in zip(fx, fy)], [p + scale * q for p, q in zip(gx_, gy_)]

    def shift(x):
        fs = [zero] + x[0]
        gs = [zc] + x[1]
        for i, e in enumerate(x[0]):
            fs[i] = fs[i] + THETA * e
        for i, e in enumerate(x[1]):
            if i:
                gs[i] = gs[i] + THETA * e
        return fs, gs

    one = jnp.ones((1, 1), F32)
    r = ([one], [zc, -c])
    x = ([zero], [c])
    p = combine(r, -one, ([zero], [q0]))
    x = combine(x, al0, p)
    r = combine(r, -al0, shift(p))
    p = combine(combine(r, -one, ([zero], [q1])), be1, p)
    x = combine(x, al1, p)
    r = combine(r, -al1, shift(p))
    p = combine(combine(r, -one, ([zero], [q2])), be2, p)
    x = combine(x, al2, p)
    r = combine(r, -al2, shift(p))

    def column_of(v):
        fs = list(v[0]) + [zero] * (4 - len(v[0]))
        gs = list(v[1]) + [zc] * (NL - len(v[1]))
        s8 = lax.broadcasted_iota(jnp.int32, (16, 128), 0)
        tail = jnp.zeros((16, 128), F32)
        for i, e in enumerate(fs):
            tail = jnp.where((s8 == i) | (s8 == 4 + i), e, tail)
        return [jnp.broadcast_to(g, (K, 128)) for g in gs] + [tail]

    cx = column_of(x)
    cr = column_of(r)
    for y in range(R):
        for t in range(C // 128):
            ln = pl.ds(128 * t, 128)
            tx = jnp.zeros((K, 128), F32)
            tr = jnp.zeros((K, 128), F32)
            for i in range(NL + 1):
                z = zbuf[t, pl.ds(Z * y + i * K, K), :]
                tx = tx + cx[i] * z
                tr = tr + cr[i] * z
            x_out[pl.ds(y, 1), ln] = st_x0[pl.ds(y, 1), ln] + jnp.sum(tx, axis=0, keepdims=True)
            r_out[pl.ds(y, 1), ln] = jnp.sum(tr, axis=0, keepdims=True)


def solution(mesh):
    n_lat, n_lon = mesh.shape["lat"], mesh.shape["lon"]

    def shards(right_side, first_guess, cell_mask, cond_east, cond_north, surface, recycled):
        K, R, C = recycled.shape
        RE, CE, S, Z = R + 2 * H, C + 128, 24, (H + 1) * K + 16
        block = jax.ShapeDtypeStruct((R, C), F32)
        vm = pltpu.VMEM
        dma = pltpu.SemaphoreType.DMA
        return pl.pallas_call(
            functools.partial(kernel, n_lat, n_lon, K, R, C),
            out_shape=(block, block),
            in_specs=[pl.BlockSpec(memory_space=pl.ANY)] * 7,
            out_specs=(pl.BlockSpec(memory_space=pltpu.VMEM),) * 2,
            scratch_shapes=[
                vm((C // 128, K * R, 128), F32),
                vm((R, C), F32), vm((R, C), F32), vm((R, C), jnp.int32),
                vm((R, C), F32), vm((R, C), F32), vm((R, C), F32),
                vm((CE // 128, S * RE, 128), F32),
                vm((CE // 128, Z * RE, 128), F32),
                vm((5, RE, CE), F32),
                vm((S, 128), F32),
                vm((6, S, 128), F32),
                vm((K, 128), F32),
                vm((n_lat, K, 128), F32),
                vm((n_lon, K, 128), F32),
                dma((6 + C // 128,)), dma((8,)), dma((8,)),
                dma((n_lat,)), dma((n_lat,)), dma((n_lon,)), dma((n_lon,)),
            ],
            compiler_params=pltpu.CompilerParams(
                collective_id=0, has_side_effects=True, vmem_limit_bytes=48 * 1024 * 1024
            ),
        )(
            right_side, first_guess, cell_mask, cond_east, cond_north, surface,
            recycled.reshape(K * R, C),
        )

    spec = P("lat", "lon")
    return jax.shard_map(
        shards,
        mesh=mesh,
        in_specs=(spec,) * 6 + (P(None, "lat", "lon"),),
        out_specs=(spec, spec),
        check_vma=False,
    )
```

time: 246 us -> 43.4 us (0.18)
  blocking collectives: 161 us -> 0 us
  Pallas kernels: 0 us -> 35.2 us
  starting transfers between devices: 26.6 us -> 0 us
  waiting for transfers between devices: 21.1 us -> 0 us
  matrix products: 13 us -> 0 us
  other arithmetic: 9.43 us -> 0 us
  between operations: 9.36 us -> 0.66 us
  local copies, waits for them, and re-layouts: 3.82 us -> 6.98 us
    psum x4 -> x0, blocking collectives: 161 us -> none  [the longest x3 121 us: shards(): lax.psum((jnp.sum(residual * residual), jnp.sum(residual * image_res), de...]
    pallas_call x0 -> x1, Pallas kernels: none -> 35.2 us  [shards(): pl.pallas_call(functools.partial(kernel, n_lat, n_lon, K, R, C), out_shap...]
    ppermute x16 -> x0, starting transfers between devices: 26.6 us -> none  [the longest x8 22 us: with_halo(): lax.ppermute(lax.slice_in_dim(block, 0, width, axis=dim), axis, backward)]
    ppermute x16 -> x0, waiting for transfers between devices: 21.1 us -> none  [the longest x8 13.5 us: with_halo(): lax.ppermute(lax.slice_in_dim(block, block.shape[dim] - width, None, axis...]
    dot_general x13 -> x0, matrix products: 9.97 us -> none  [the longest x3 2.84 us: shards(): defl_local = jnp.einsum('kyx,yx->k', recycled, image_res, precision=PRECISE)]
    unnamed x15 -> x16, local copies, waits for them, and re-layouts: 2.45 us -> 6.98 us
    another operation x5 -> x0, other arithmetic: 4.01 us -> none  [the longest x3 2.13 us: shards(): factor = jnp.linalg.cholesky(0.5 * (gram + gram.T))]
    another operation x8 -> x0, matrix products: 3.05 us -> none  [solve_small(): return jax.scipy.linalg.cho_solve((factor, True), target)]
  transfers between devices with their start and end apart: 16 -> 0, of which waited for: 12 -> 0; matrix products, arithmetic and copies ran while one was open for 1% -> 0% of each run, Pallas kernels for 0% -> 0%
where the time goes in v1:
time: 43.4 us; the launch traced here: 42.9 us
  Pallas kernels  35.2 us (81%)
  local copies, waits for them, and re-layouts  6.98 us (16%)
  between operations  0.66 us (2%)
    pallas_call x1, Pallas kernels, shards(): pl.pallas_call(functools.partial(kernel, n_lat, n_lon, K, R, C), out_shap...  35.2 us
    unnamed x16, local copies, waits for them, and re-layouts  6.98 us

profile of v1, /device:TPU:0, one launch (start us, length us, event | category | flops | bytes accessed | tf_op | source)
XLA Modules:
  0.0 42.9 jit_solution(18330726934303986798)
XLA Ops:
  0.6 0.0 copy-start
  0.6 1.1 %copy-done = f32[16,16,640]{2,1,0:T(8,128)S(1)} copy-done((f32[16,16,640]{2,1,0:T(8,128)S(1)}, f32[16,16,640]{2,1,0:T(8,128)}, u32[]{:S(2)}) %copy-start) | copy-done | bytes 655384
  1.7 0.0 copy-start.1
  1.7 0.8 %copy-done.1 = f32[16,640]{1,0:T(8,128)S(1)} copy-done((f32[16,640]{1,0:T(8,128)S(1)}, f32[16,640]{1,0:T(8,128)}, u32[]{:S(2)}) %copy-start.1) | copy-done | bytes 40984
  2.5 0.0 copy-start.2
  2.5 0.8 %copy-done.2 = f32[16,640]{1,0:T(8,128)S(1)} copy-done((f32[16,640]{1,0:T(8,128)S(1)}, f32[16,640]{1,0:T(8,128)}, u32[]{:S(2)}) %copy-start.2) | copy-done | bytes 40984
  3.3 0.0 copy-start.3
  3.3 0.8 %copy-done.3 = s32[16,640]{1,0:T(8,128)S(1)} copy-done((s32[16,640]{1,0:T(8,128)S(1)}, s32[16,640]{1,0:T(8,128)}, u32[]{:S(2)}) %copy-start.3) | copy-done | bytes 40984
  4.1 0.0 copy-start.4
  4.1 0.8 %copy-done.4 = f32[16,640]{1,0:T(8,128)S(1)} copy-done((f32[16,640]{1,0:T(8,128)S(1)}, f32[16,640]{1,0:T(8,128)}, u32[]{:S(2)}) %copy-start.4) | copy-done | bytes 40984
  4.8 0.0 copy-start.5
  4.8 0.8 %copy-done.5 = f32[16,640]{1,0:T(8,128)S(1)} copy-done((f32[16,640]{1,0:T(8,128)S(1)}, f32[16,640]{1,0:T(8,128)}, u32[]{:S(2)}) %copy-start.5) | copy-done | bytes 40984
  5.6 0.0 copy-start.6
  5.6 0.8 %copy-done.6 = f32[16,640]{1,0:T(8,128)S(1)} copy-done((f32[16,640]{1,0:T(8,128)S(1)}, f32[16,640]{1,0:T(8,128)}, u32[]{:S(2)}) %copy-start.6) | copy-done | bytes 40984
  6.4 35.2 %shard_map.86 = (f32[16,640]{1,0:T(8,128)S(1)}, f32[16,640]{1,0:T(8,128)S(1)}) custom-call(f32[16,640]{1,0:T(8,128)S(1)} %copy-done.1, f32[16,640]{1,0:T(8,128)S(1)} %copy-done.2, s32[16,640]{1,0:T(8,128)S(1)} %copy-done.3, f32[16,640]{1,0:T(8,128)S(1)} %copy-done.4, f32[16,640]{1,0:T(8,128)S(1)} %copy-done.5, f32[16,640]{1,0:T(8,128)S(1)} %copy-done.6, ...), custom_call_target="tpu_custom_call" | custom-call | tf_op jit(solution)/shard_map/pallas_call | solution.py:507
  41.6 0.6 %copy.11 = f32[16,640]{1,0:T(8,128)} copy(f32[16,640]{1,0:T(8,128)S(1)} %get-tuple-element.4) | data formatting | bytes 81920
  42.2 0.6 %copy.12 = f32[16,640]{1,0:T(8,128)} copy(f32[16,640]{1,0:T(8,128)S(1)} %get-tuple-element.5) | data formatting | bytes 81920
Async XLA Ops:
  0.6 1.1 %copy-start = (f32[16,16,640]{2,1,0:T(8,128)S(1)}, f32[16,16,640]{2,1,0:T(8,128)}, u32[]{:S(2)}) copy-start(f32[16,16,640]{2,1,0:T(8,128)} %param.13) | copy-start | bytes 1966084
  1.7 0.8 %copy-start.1 = (f32[16,640]{1,0:T(8,128)S(1)}, f32[16,640]{1,0:T(8,128)}, u32[]{:S(2)}) copy-start(f32[16,640]{1,0:T(8,128)} %b_hbm.1) | copy-start | bytes 122884
  2.5 0.8 %copy-start.2 = (f32[16,640]{1,0:T(8,128)S(1)}, f32[16,640]{1,0:T(8,128)}, u32[]{:S(2)}) copy-start(f32[16,640]{1,0:T(8,128)} %x0_hbm.1) | copy-start | bytes 122884
  3.3 0.8 %copy-start.3 = (s32[16,640]{1,0:T(8,128)S(1)}, s32[16,640]{1,0:T(8,128)}, u32[]{:S(2)}) copy-start(s32[16,640]{1,0:T(8,128)} %mask_hbm.1) | copy-start | bytes 122884
  4.1 0.8 %copy-start.4 = (f32[16,640]{1,0:T(8,128)S(1)}, f32[16,640]{1,0:T(8,128)}, u32[]{:S(2)}) copy-start(f32[16,640]{1,0:T(8,128)} %ce_hbm.1) | copy-start | bytes 122884
  4.8 0.8 %copy-start.5 = (f32[16,640]{1,0:T(8,128)S(1)}, f32[16,640]{1,0:T(8,128)}, u32[]{:S(2)}) copy-start(f32[16,640]{1,0:T(8,128)} %cn_hbm.1) | copy-start | bytes 122884
  5.6 0.8 %copy-start.6 = (f32[16,640]{1,0:T(8,128)S(1)}, f32[16,640]{1,0:T(8,128)}, u32[]{:S(2)}) copy-start(f32[16,640]{1,0:T(8,128)} %surf_hbm.1) | copy-start | bytes 122884

commit v2 on v1

--- a/solution.py
+++ b/solution.py
@@ -19,7 +19,7 @@
     b_hbm, x0_hbm, mask_hbm, ce_hbm, cn_hbm, surf_hbm, w_hbm,
     x_out, r_out,
     stage_w, st_b, st_x0, st_mask, st_ce, st_cn, st_surf,
-    ext, zbuf, coef, pack, packs_in, part, red1, red2,
+    ext, zbuf, coef, pack, packs_in, gram_acc, part, red1, red2,
     load_sem, send_sem, recv_sem, s1_send, s1_recv, s2_send, s2_recv,
 ):
     lat = lax.axis_index("lat")
@@ -140,28 +140,6 @@
     to_e.wait()
     to_w.wait()
 
-    @pl.when(has_n)
-    def _():
-        for c in to_n:
-            c.wait_send()
-        for c in to_s:
-            c.wait_recv()
-
-    @pl.when(has_s)
-    def _():
-        for c in to_s:
-            c.wait_send()
-        for c in to_n:
-            c.wait_recv()
-
-    @pl.when(jnp.logical_not(has_n))
-    def _():
-        ext[:, pl.ds(S * R, S * H), :] = jnp.zeros((CE // 128, S * H, 128), F32)
-
-    @pl.when(jnp.logical_not(has_s))
-    def _():
-        ext[:, pl.ds(S * (R + H), S * H), :] = jnp.zeros((CE // 128, S * H, 128), F32)
-
     def unpack(y_ext, y_src, west_slot, east_slot, keep):
         from_e = packs_in[east_slot]
         from_w = packs_in[west_slot]
@@ -174,14 +152,6 @@
 
     for y in range(R):
         unpack(y, y, 0, 1, None)
-    for y in range(H):
-        unpack(R + y, y, 4, 5, has_n)
-        unpack(R + H + y, R - H + y, 2, 3, has_s)
-
-    def field(f):
-        return jnp.concatenate(
-            [ext[t, pl.ds(K + f, RE, stride=S), :] for t in range(CE // 128)], axis=1
-        )
 
     def e_of(v):
         return pltpu.roll(v, CE - 1, 1)
@@ -189,69 +159,66 @@
     def w_of(v):
         return pltpu.roll(v, 1, 1)
 
-    def n_of(v):
-        return pltpu.roll(v, RE - 1, 0)
-
-    def s_of(v):
-        return pltpu.roll(v, 1, 0)
-
-    x0 = field(0)
-    rhs = field(1)
-    wet = field(2)
-    cew = field(3) * wet
-    cnw = field(4) * wet
-    k_e = cew * e_of(wet)
-    k_w = w_of(cew) * wet
-    k_n = cnw * n_of(wet)
-    k_s = s_of(cnw) * wet
-    centre = field(5) * wet + k_e + k_w + k_n + k_s + (1.0 - wet)
-    for i, v in enumerate((centre, k_e, k_w, k_n, k_s)):
-        coef[i] = v
-
-    def operate(v):
-        return centre * v - (k_e * e_of(v) + k_w * w_of(v) + k_n * n_of(v) + k_s * s_of(v))
-
-    s_fam = [rhs - operate(x0)]
-    for _ in range(ITERS):
-        s_fam.append(operate(s_fam[-1]) - THETA * s_fam[-1])
-    for t in range(C // 128):
-        ln = pl.ds(128 * t, 128)
-        for i, v in enumerate(s_fam):
-            p = v[:R, 128 * t:128 * t + 128]
-            p_hi = p.astype(jnp.bfloat16).astype(F32)
-            zbuf[t, pl.ds(NL * K + i, R, stride=Z), :] = p_hi
-            zbuf[t, pl.ds(NL * K + 4 + i, R, stride=Z), :] = p - p_hi
-        for i in range(8, 16):
-            zbuf[t, pl.ds(NL * K + i, R, stride=Z), :] = jnp.zeros((R, 128), F32)
-
-    def rows(ref, level, y):
-        start = S * y if level == 0 else Z * y + level * K
-        at = pl.ds(pl.multiple_of(start, 8), K)
+    def base(n, level):
+        def field(f):
+            return jnp.concatenate(
+                [ext[t, pl.ds(K + f, n, stride=S), :] for t in range(CE // 128)], axis=1
+            )
+
+        def n_of(v):
+            return pltpu.roll(v, n - 1, 0)
+
+        def s_of(v):
+            return pltpu.roll(v, 1, 0)
+
+        x0 = field(0)
+        rhs = field(1)
+        wet = field(2)
+        cew = field(3) * wet
+        cnw = field(4) * wet
+        k_e = cew * e_of(wet)
+        k_w = w_of(cew) * wet
+        k_n = cnw * n_of(wet)
+        k_s = s_of(cnw) * wet
+        centre = field(5) * wet + k_e + k_w + k_n + k_s + (1.0 - wet)
+        for i, v in enumerate((centre, k_e, k_w, k_n, k_s)):
+            coef[i, 0:n] = v
+
+        def operate(v):
+            return centre * v - (k_e * e_of(v) + k_w * w_of(v) + k_n * n_of(v) + k_s * s_of(v))
+
+        s_fam = [rhs - operate(x0)]
+        for _ in range(ITERS):
+            s_fam.append(operate(s_fam[-1]) - THETA * s_fam[-1])
+        for t in range(C // 128):
+            for i, v in enumerate(s_fam):
+                p = v[:R, 128 * t:128 * t + 128]
+                p_hi = p.astype(jnp.bfloat16).astype(F32)
+                zbuf[t, pl.ds(NL * K + i, R, stride=Z), :] = p_hi
+                zbuf[t, pl.ds(NL * K + 4 + i, R, stride=Z), :] = p - p_hi
+            if level == 0:
+                for i in range(8, 16):
+                    zbuf[t, pl.ds(NL * K + i, R, stride=Z), :] = jnp.zeros((R, 128), F32)
+
+    def rows(level, y):
+        y = y % RE
+        ref = ext if level == 0 else zbuf
+        at = pl.ds(S * y if level == 0 else Z * y + level * K, K)
         return jnp.concatenate([ref[t, at, :] for t in range(CE // 128)], axis=1)
 
-    for level in range(1, NL):
-        h = NL - 1 - level
-        src = ext if level == 1 else zbuf
-
-        def body(t, _, level=level, h=h, src=src):
-            y = lax.rem(t + (RE - h), RE)
-            yn = lax.rem(y + 1, RE)
-            ys = lax.rem(y + RE - 1, RE)
-            v = rows(src, level - 1, y)
-            vn = rows(src, level - 1, yn)
-            vs = rows(src, level - 1, ys)
-
-            def kk(i):
-                return coef[i, pl.ds(y, 1), :]
-
-            diag = kk(0) if level == 1 else kk(0) - THETA
-            out = diag * v - (kk(1) * e_of(v) + kk(2) * w_of(v) + kk(3) * vn + kk(4) * vs)
-            at = pl.ds(pl.multiple_of(Z * y + level * K, 8), K)
-            for u in range(CE // 128):
-                zbuf[u, at, :] = out[:, 128 * u:128 * u + 128]
-            return 0
-
-        lax.fori_loop(0, R + 2 * h, body, 0)
+    def step(level, y):
+        v = rows(level - 1, y)
+        vn = rows(level - 1, y + 1)
+        vs = rows(level - 1, y - 1)
+
+        def kk(i):
+            return coef[i, pl.ds(y % RE, 1), :]
+
+        diag = kk(0) if level == 1 else kk(0) - THETA
+        out = diag * v - (kk(1) * e_of(v) + kk(2) * w_of(v) + kk(3) * vn + kk(4) * vs)
+        at = pl.ds(Z * (y % RE) + level * K, K)
+        for u in range(CE // 128):
+            zbuf[u, at, :] = out[:, 128 * u:128 * u + 128]
 
     def gram_step(t, total):
         z = jnp.concatenate(
@@ -268,7 +235,45 @@
             both, both, (((1,), (1,)), ((), ())), preferred_element_type=F32
         )
 
-    G = lax.fori_loop(0, R // 2, gram_step, jnp.zeros((Z + NL * K, Z + NL * K), F32))
+    base(R, 0)
+    for level in range(1, NL):
+        for y in range(level, R - level):
+            step(level, y)
+    G = jnp.zeros((Z + NL * K, Z + NL * K), F32)
+    gram_acc[...] = lax.fori_loop(H // 2, (R - H) // 2, gram_step, G)
+
+    @pl.when(has_n)
+    def _():
+        for c in to_n:
+            c.wait_send()
+        for c in to_s:
+            c.wait_recv()
+
+    @pl.when(has_s)
+    def _():
+        for c in to_s:
+            c.wait_send()
+        for c in to_n:
+            c.wait_recv()
+
+    @pl.when(jnp.logical_not(has_n))
+    def _():
+        ext[:, pl.ds(S * R, S * H), :] = jnp.zeros((CE // 128, S * H, 128), F32)
+
+    @pl.when(jnp.logical_not(has_s))
+    def _():
+        ext[:, pl.ds(S * (R + H), S * H), :] = jnp.zeros((CE // 128, S * H, 128), F32)
+
+    for y in range(H):
+        unpack(R + y, y, 4, 5, has_n)
+        unpack(R + H + y, R - H + y, 2, 3, has_s)
+    base(RE, 1)
+    for level in range(1, NL):
+        h = NL - 1 - level
+        for y in list(range(-h, level)) + list(range(R - level, R + h)):
+            step(level, y)
+    G = lax.fori_loop(0, H // 2, gram_step, gram_acc[...])
+    G = lax.fori_loop((R - H) // 2, R // 2, gram_step, G)
     zl = jnp.zeros((Z + NL * K, 256 - Z - NL * K), F32)
     G = jnp.concatenate([G, zl], axis=1)
     GL = pltpu.roll(G, 256 - Z, 1)[:, :128]
@@ -507,7 +512,7 @@
         return pl.pallas_call(
             functools.partial(kernel, n_lat, n_lon, K, R, C),
             out_shape=(block, block),
-            in_specs=[pl.BlockSpec(memory_space=pl.ANY)] * 7,
+            in_specs=[pl.BlockSpec(memory_space=pltpu.HBM)] * 7,
             out_specs=(pl.BlockSpec(memory_space=pltpu.VMEM),) * 2,
             scratch_shapes=[
                 vm((C // 128, K * R, 128), F32),
@@ -518,6 +523,7 @@
                 vm((5, RE, CE), F32),
                 vm((S, 128), F32),
                 vm((6, S, 128), F32),
+                vm((Z + (H + 1) * K, Z + (H + 1) * K), F32),
                 vm((K, 128), F32),
                 vm((n_lat, K, 128), F32),
                 vm((n_lon, K, 128), F32),
@@ -525,7 +531,7 @@
                 dma((n_lat,)), dma((n_lat,)), dma((n_lon,)), dma((n_lon,)),
             ],
             compiler_params=pltpu.CompilerParams(
-                collective_id=0, has_side_effects=True, vmem_limit_bytes=48 * 1024 * 1024
+                collective_id=0, has_side_effects=True, vmem_limit_bytes=67043328
             ),
         )(
             right_side, first_guess, cell_mask, cond_east, cond_north, surface,

time: 43.4 us -> 30.3 us (0.70)
  Pallas kernels: 35.2 us -> 27.4 us
  local copies, waits for them, and re-layouts: 6.98 us -> 2.03 us
    pallas_call x1, Pallas kernels: 35.2 us -> 27.4 us  [shards(): pl.pallas_call(functools.partial(kernel, n_lat, n_lon, K, R, C), out_shap...]
    unnamed x16 -> x4, local copies, waits for them, and re-layouts: 6.98 us -> 2.03 us
where the time goes in v2:
time: 30.3 us; the launch traced here: 30.1 us
  Pallas kernels  27.4 us (90%)
  local copies, waits for them, and re-layouts  2.03 us (7%)
  between operations  0.65 us (2%)
    pallas_call x1, Pallas kernels, shards(): pl.pallas_call(functools.partial(kernel, n_lat, n_lon, K, R, C), out_shap...  27.4 us
    unnamed x4, local copies, waits for them, and re-layouts  2.03 us

profile of v2, /device:TPU:0, one launch (start us, length us, event | category | flops | bytes accessed | tf_op | source)
XLA Modules:
  0.0 30.1 jit_solution(5183388929036377093)
XLA Ops:
  0.6 27.4 %shard_map.86 = (f32[16,640]{1,0:T(8,128)}, f32[16,640]{1,0:T(8,128)}) custom-call(f32[16,640]{1,0:T(8,128)} %b_hbm.1, f32[16,640]{1,0:T(8,128)} %x0_hbm.1, s32[16,640]{1,0:T(8,128)} %mask_hbm.1, f32[16,640]{1,0:T(8,128)} %ce_hbm.1, f32[16,640]{1,0:T(8,128)} %cn_hbm.1, f32[16,640]{1,0:T(8,128)} %surf_hbm.1, f32[256,640]{1,0:T(8,128)} %bitcast.1), custom_call_target="tpu_custom_call" | custom-call | tf_op jit(solution)/shard_map/pallas_call | solution.py:512
  28.1 0.0 copy-start
  28.1 1.4 %copy.11 = f32[16,640]{1,0:T(8,128)} copy(f32[16,640]{1,0:T(8,128)} %get-tuple-element.4) | data formatting | bytes 81920
  29.5 0.0 copy-done
  29.5 0.6 %copy.12 = f32[16,640]{1,0:T(8,128)} copy(f32[16,640]{1,0:T(8,128)S(1)} %copy-done) | data formatting | bytes 81920
Async XLA Ops:
  28.1 1.4 %copy-start = (f32[16,640]{1,0:T(8,128)S(1)}, f32[16,640]{1,0:T(8,128)}, u32[]{:S(2)}) copy-start(f32[16,640]{1,0:T(8,128)} %get-tuple-element.5) | copy-start | bytes 122884

commit v3 on v2

--- a/solution.py
+++ b/solution.py
@@ -17,7 +17,7 @@
 def kernel(
     n_lat, n_lon, K, R, C,
     b_hbm, x0_hbm, mask_hbm, ce_hbm, cn_hbm, surf_hbm, w_hbm,
-    x_out, r_out,
+    out,
     stage_w, st_b, st_x0, st_mask, st_ce, st_cn, st_surf,
     ext, zbuf, coef, pack, packs_in, gram_acc, part, red1, red2,
     load_sem, send_sem, recv_sem, s1_send, s1_recv, s2_send, s2_recv,
@@ -496,8 +496,8 @@
                 z = zbuf[t, pl.ds(Z * y + i * K, K), :]
                 tx = tx + cx[i] * z
                 tr = tr + cr[i] * z
-            x_out[pl.ds(y, 1), ln] = st_x0[pl.ds(y, 1), ln] + jnp.sum(tx, axis=0, keepdims=True)
-            r_out[pl.ds(y, 1), ln] = jnp.sum(tr, axis=0, keepdims=True)
+            out[pl.ds(y, 1), ln] = st_x0[pl.ds(y, 1), ln] + jnp.sum(tx, axis=0, keepdims=True)
+            out[pl.ds(R + y, 1), ln] = jnp.sum(tr, axis=0, keepdims=True)
 
 
 def solution(mesh):
@@ -506,14 +506,14 @@
     def shards(right_side, first_guess, cell_mask, cond_east, cond_north, surface, recycled):
         K, R, C = recycled.shape
         RE, CE, S, Z = R + 2 * H, C + 128, 24, (H + 1) * K + 16
-        block = jax.ShapeDtypeStruct((R, C), F32)
+        block = jax.ShapeDtypeStruct((2 * R, C), F32)
         vm = pltpu.VMEM
         dma = pltpu.SemaphoreType.DMA
-        return pl.pallas_call(
+        both = pl.pallas_call(
             functools.partial(kernel, n_lat, n_lon, K, R, C),
-            out_shape=(block, block),
+            out_shape=block,
             in_specs=[pl.BlockSpec(memory_space=pltpu.HBM)] * 7,
-            out_specs=(pl.BlockSpec(memory_space=pltpu.VMEM),) * 2,
+            out_specs=pl.BlockSpec(memory_space=pltpu.VMEM),
             scratch_shapes=[
                 vm((C // 128, K * R, 128), F32),
                 vm((R, C), F32), vm((R, C), F32), vm((R, C), jnp.int32),
@@ -537,6 +537,7 @@
             right_side, first_guess, cell_mask, cond_east, cond_north, surface,
             recycled.reshape(K * R, C),
         )
+        return both[:R], both[R:]
 
     spec = P("lat", "lon")
     return jax.shard_map(

time: 30.3 us -> 29.7 us (0.980)
  local copies, waits for them, and re-layouts: 2.03 us -> 1.43 us
    unnamed x4 -> x0, local copies, waits for them, and re-layouts: 2.03 us -> none
    slice x0 -> x1, local copies, waits for them, and re-layouts: none -> 1.43 us  [shards(): return (both[:R], both[R:])]
where the time goes in v3:
time: 29.7 us; the launch traced here: 29.5 us
  Pallas kernels  27.4 us (92%)
  local copies, waits for them, and re-layouts  1.43 us (5%)
  between operations  0.64 us (2%)
    pallas_call x1, Pallas kernels, shards(): pl.pallas_call(functools.partial(kernel, n_lat, n_lon, K, R, C), out_shap...  27.4 us
    slice x1, local copies, waits for them, and re-layouts, shards(): return (both[:R], both[R:])  1.43 us

profile of v3, /device:TPU:0, one launch (start us, length us, event | category | flops | bytes accessed | tf_op | source)
XLA Modules:
  0.0 29.5 jit_solution(17707990839032997248)
XLA Ops:
  0.6 27.4 %shard_map.86 = f32[32,640]{1,0:T(8,128)} custom-call(f32[16,640]{1,0:T(8,128)} %b_hbm.1, f32[16,640]{1,0:T(8,128)} %x0_hbm.1, s32[16,640]{1,0:T(8,128)} %mask_hbm.1, f32[16,640]{1,0:T(8,128)} %ce_hbm.1, f32[16,640]{1,0:T(8,128)} %cn_hbm.1, f32[16,640]{1,0:T(8,128)} %surf_hbm.1, f32[256,640]{1,0:T(8,128)} %bitcast.1), custom_call_target="tpu_custom_call" | custom-call | tf_op jit(solution)/shard_map/pallas_call | solution.py:512
  28.0 1.4 %fusion = (f32[16,640]{1,0:T(8,128)}, f32[16,640]{1,0:T(8,128)}) fusion(f32[32,640]{1,0:T(8,128)} %shard_map.86), kind=kLoop, calls=%fused_computation | loop fusion | bytes 163840 | tf_op jit(solution)/shard_map/slice | solution.py:540
